TPU v7x, 32 devices: a whole 2x2x4 slice. The times are simulated.
32 devices in a mesh: rad: 8 (over y, x, core), ang: 4 (over z).
Axes of the slice: x: 2, y: 2, z: 4, core: 2. Of those that a mesh axis runs over, the one named last changes fastest.
Arguments:
- density: float32 [3, 512, 128, 512], P(None, 'rad', 'ang'), may hold values from -13 to 13
Outputs:
- potential: float32 [3, 512, 128, 512], P(None, 'rad', 'ang')
All inputs are finite; a program needn't handle non-finite values.
Results may differ from a plain program's by a relative error of at most 0.0003.
Values sent between devices are 32-bit elements; how exact they have to be, the bound alone decides.
A program may use at most 128 MiB of HBM per device.

v0:
```python
import math

import jax
import jax.numpy as jnp
import numpy as np
from jax import lax
from jax.sharding import PartitionSpec as P

LMAX = 12


INNER = 0.5
COUPLING = 2000.0


def entering(part, axis, combine, identity, reverse):
    count = lax.axis_size(axis)
    place = lax.axis_index(axis)
    ahead = count - 1 - place if reverse else place
    gathered = lax.all_gather(part, axis)
    state = jnp.zeros_like(part) + jnp.asarray(identity, part.dtype)

    def one(turn, state):
        source = count - 1 - turn if reverse else turn
        return combine(state, lax.dynamic_index_in_dim(gathered, source, 0, False))

    return lax.fori_loop(0, ahead, one, state)


def legendre_table(polar_angle):
    cos_theta = jnp.cos(polar_angle)
    sine_theta = jnp.sin(polar_angle)
    values_lm = {}
    values_lm[0, 0] = jnp.full_like(polar_angle, 1.0 / math.sqrt(4.0 * math.pi))
    for m in range(1, LMAX + 1):
        values_lm[m, m] = (
            math.sqrt((2.0 * m + 1.0) / (2.0 * m)) * sine_theta * values_lm[m - 1, m - 1]
        )
    for m in range(0, LMAX):
        values_lm[m + 1, m] = math.sqrt(2.0 * m + 3.0) * cos_theta * values_lm[m, m]
    for m in range(0, LMAX + 1):
        for l in range(m + 2, LMAX + 1):
            coef_a = math.sqrt((4.0 * l * l - 1.0) / (l * l - m * m))
            coef_b = math.sqrt(((l - 1.0) ** 2 - m * m) / (4.0 * (l - 1.0) ** 2 - 1.0))
            values_lm[l, m] = coef_a * (
                cos_theta * values_lm[l - 1, m] - coef_b * values_lm[l - 2, m]
            )
    degree_rows = []
    for l in range(LMAX + 1):
        columns = []
        for k in range(2 * LMAX + 1):
            m = (k + 1) // 2
            columns.append(values_lm[l, m] if m <= l else jnp.zeros_like(polar_angle))
        degree_rows.append(jnp.stack(columns, -1))
    return jnp.stack(degree_rows, 1)


def fourier_table(phi_cells):
    azimuth = jnp.arange(phi_cells, dtype=jnp.float32) * (2.0 * math.pi / phi_cells)
    column = jnp.arange(2 * LMAX + 1)
    order_m = ((column + 1) // 2).astype(jnp.float32)
    phase = azimuth[:, None] * order_m[None, :]
    root_two = math.sqrt(2.0)
    return jnp.where(
        column[None, :] == 0,
        jnp.ones_like(phase),
        jnp.where(column[None, :] % 2 == 1, root_two * jnp.cos(phase), root_two * jnp.sin(phase)),
    )


def slot_selector():
    width = 2 * LMAX + 1
    used = [l * width + k for l in range(LMAX + 1) for k in range(width) if (k + 1) // 2 <= l]
    table = np.zeros(((LMAX + 1) * width, len(used)), np.float32)
    table[np.array(used), np.arange(len(used))] = 1.0
    return jnp.asarray(table)


def add_terms(earlier, later):
    return jax.tree.map(jnp.add, earlier, later)


def body(density):
    snapshots, shells, theta_rows, phi_cells = density.shape
    width = 2 * LMAX + 1
    total_shells = shells * lax.axis_size("rad")
    total_rows = theta_rows * lax.axis_size("ang")
    row_index = lax.axis_index("ang") * theta_rows + jnp.arange(theta_rows, dtype=jnp.int32)
    polar_angle = (row_index.astype(jnp.float32) + 0.5) * (math.pi / total_rows)
    legendre = legendre_table(polar_angle)
    weights = jnp.sin(polar_angle) * (math.pi / total_rows) * (2.0 * math.pi / phi_cells)
    fourier = fourier_table(phi_cells)
    spacing = (1.0 - INNER) / total_shells
    shell_index = lax.axis_index("rad") * shells + jnp.arange(shells, dtype=jnp.int32)
    radius = INNER + (shell_index.astype(jnp.float32) + 0.5) * spacing
    azimuthal = jnp.dot(
        density.reshape(snapshots * shells * theta_rows, phi_cells),
        fourier,
        precision=lax.Precision.HIGHEST,
        preferred_element_type=jnp.float32,
    )
    azimuthal = azimuthal.reshape(snapshots, shells, theta_rows, width)
    partial_moments = jnp.einsum(
        "frtk,tlk->frlk",
        azimuthal,
        legendre * weights[:, None, None],
        precision=lax.Precision.HIGHEST,
    )
    selector = slot_selector()
    packed = jnp.dot(
        partial_moments.reshape(snapshots * shells, (LMAX + 1) * width),
        selector,
        precision=lax.Precision.HIGHEST,
        preferred_element_type=jnp.float32,
    )
    summed = lax.psum(packed, "ang")
    moments = jnp.dot(
        summed, selector.T, precision=lax.Precision.HIGHEST, preferred_element_type=jnp.float32
    ).reshape(snapshots, shells, LMAX + 1, width)
    degree = jnp.arange(LMAX + 1, dtype=jnp.float32)
    inner_terms = moments * (radius[:, None] ** (degree + 2.0) * spacing)[None, :, :, None]
    outer_terms = moments * (radius[:, None] ** (1.0 - degree) * spacing)[None, :, :, None]
    inner_total = jnp.sum(inner_terms, 1)
    outer_total = jnp.sum(outer_terms, 1)
    zeros_block = jnp.zeros_like(inner_total)
    from_below = entering(inner_total, "rad", add_terms, zeros_block, False)
    from_above = entering(outer_total, "rad", add_terms, zeros_block, True)
    inner_sum = from_below[:, None] + jnp.cumsum(inner_terms, 1) - 0.5 * inner_terms
    outer_sum = (
        from_above[:, None]
        + jnp.flip(jnp.cumsum(jnp.flip(outer_terms, 1), 1), 1)
        - 0.5 * outer_terms
    )
    factor = (-COUPLING * 4.0 * math.pi / (2.0 * degree + 1.0))[None, None, :, None]
    coefficient = factor * (
        (radius[:, None] ** (-(degree[None, :] + 1.0)))[None, :, :, None] * inner_sum
        + (radius[:, None] ** degree[None, :])[None, :, :, None] * outer_sum
    )
    spread = jnp.einsum("frlk,tlk->frtk", coefficient, legendre, precision=lax.Precision.HIGHEST)
    potential = jnp.dot(
        spread.reshape(snapshots * shells * theta_rows, width),
        fourier.T,
        precision=lax.Precision.HIGHEST,
        preferred_element_type=jnp.float32,
    )
    return potential.reshape(snapshots, shells, theta_rows, phi_cells)


def solution(mesh):
    return jax.shard_map(
        body,
        mesh=mesh,
        in_specs=(P(None, "rad", "ang", None),),
        out_specs=P(None, "rad", "ang", None),
        check_vma=False,
    )
```

profile of v0, /device:TPU:0, one launch (start us, length us, event | category | flops | bytes accessed | tf_op | source)
XLA Modules:
  0.0 137.9 jit_solution(15535400083472716511)
XLA Ops:
  6.5 0.6 sine_multiply_fusion
  7.2 0.1 broadcast_multiply_fusion.4
  7.2 0.1 subtract_multiply_fusion.12
  7.3 0.1 subtract_multiply_fusion.2
  7.8 0.1 subtract_multiply_fusion.10
  7.9 0.1 broadcast_multiply_fusion.6
  8.0 0.1 subtract_multiply_fusion.4
  8.1 0.1 broadcast_multiply_fusion.28
  8.2 0.1 broadcast_multiply_fusion.12
  8.3 0.1 subtract_multiply_fusion.6
  8.7 0.1 subtract_multiply_fusion.8
  8.9 0.1 broadcast_multiply_fusion.30
  9.0 0.1 broadcast_multiply_fusion.8
  9.2 0.1 subtract_multiply_fusion.20
  9.2 0.1 subtract_multiply_fusion.18
  9.3 0.1 broadcast_multiply_fusion.14
  9.4 0.1 broadcast_multiply_fusion.24
  9.5 0.1 broadcast_multiply_fusion.16
  9.5 0.1 subtract_multiply_fusion.16
  9.6 0.1 subtract_multiply_fusion.14
  9.7 0.1 broadcast_multiply_fusion.22
  10.2 0.1 stack.72
  10.3 0.2 stack.70
  10.5 0.2 stack.68
  10.7 0.2 stack.66
  10.9 0.1 stack.64
  11.0 0.2 stack.62
  11.3 0.2 stack.60
  11.6 0.2 stack.58
  11.8 0.2 stack.56
  12.0 0.2 stack.54
  12.3 0.2 stack.50
  12.6 0.2 stack.52
  12.8 15.4 %convolution_bitcast_fusion = f32[6144,25]{0,1:T(8,128)S(1)} fusion(f32[6144,512]{1,0:T(8,128)} %bitcast.64, f32[25]{0:T(128)S(1)} %fusion.29, f32[512]{0:T(512)S(1)} %iota_multiply_fusion, pred[25]{0:T(512)(128)(4,1)S(1)} %get-tuple-element.109, pred[25]{0:T(512)(128)(4,1)S(1)} %get-tuple-element.110), kind=kOutput, calls=%fused_computation.2 | convolution fusion | flops 943782400 | bytes 13199510 | tf_op jit(solution)/shard_map/dot_general | solution.py:96
  28.2 0.8 reshape.1258
  29.0 1.0 stack.74
  30.0 5.8 %convolution_bitcast_fusion.2 = f32[3,64,13,25]{1,2,0,3:T(8,128)S(1)} fusion(f32[3,64,32,25]{2,1,0,3:T(8,128)S(1)} %reshape.1258, f32[32,13,25]{0,1,2:T(8,128)S(1)} %stack.74, f32[32]{0:T(128)} %sine_multiply_fusion), kind=kOutput, calls=%fused_computation.8 | convolution fusion | flops 23972000 | bytes 905728 | tf_op jit(solution)/shard_map/frtk,tlk->frlk/dot_general | solution.py:103
  35.8 0.3 copy.31
  36.1 0.4 reshape.1259
  36.5 0.3 copy-done
  36.8 1.5 %fusion.37 = f32[192,169]{0,1:T(8,128)} fusion(f32[192,325]{0,1:T(8,128)S(1)} %reshape.1259, f32[325,169]{1,0:T(8,128)S(1)} %copy-done), kind=kOutput, calls=%fused_computation.198 | convolution fusion | flops 126547200 | bytes 599092 | tf_op jit(solution)/shard_map/dot_general | solution.py:110
  38.3 0.2 broadcast_power_fusion
  38.6 37.2 %all-reduce.2.cloned.1.call-done = f32[192,169]{0,1:T(8,128)} async-done(((f32[192,169]{0,1:T(8,128)}), f32[192,169]{0,1:T(8,128)}) %all-reduce.2.cloned.1.call-update) | async-done | bytes 129808 | tf_op jit(solution)/shard_map/psum | solution.py:116
  75.8 1.4 fusion.38
  77.2 0.2 reshape.1260
  77.4 0.7 copy.33
  78.1 0.4 multiply_reduce_fusion
  78.6 10.2 %all-gather = f32[24,13,25]{2,1,0:T(8,128)} all-gather(f32[3,13,25]{2,1,0:T(8,128)S(1)} %get-tuple-element.86), channel_id=2, replica_groups=mesh['rad'=8,'ang'=4] {'rad'}, dimensions={0}, use_global_device_ids=true | all-gather | bytes 35100 | tf_op jit(solution)/shard_map/all_gather | solution.py:20
  88.8 14.3 %all-gather.1 = f32[24,13,25]{2,1,0:T(8,128)} all-gather(f32[3,13,25]{2,1,0:T(8,128)S(1)} %get-tuple-element.87), channel_id=3, replica_groups=mesh['rad'=8,'ang'=4] {'rad'}, dimensions={0}, use_global_device_ids=true | all-gather | bytes 35100 | tf_op jit(solution)/shard_map/all_gather | solution.py:20
  103.1 5.2 %while.23 = (s32[]{:T(128)}, f32[3,13,25]{2,1,0:T(8,128)S(1)}, s32[]{:T(128)}, f32[8,3,13,25]{3,2,1,0:T(8,128)}, s32[]{:T(128)}, /*index=5*/s32[]{:T(128)}, s32[]{:T(128)}, s32[]{:T(128)}) while((s32[]{:T(128)}, f32[3,13,25]{2,1,0:T(8,128)S(1)}, s32[]{:T(128)}, f32[8,3,13,25]{3,2,1,0:T(8,128)}, s32[]{:T(128)}, /*index=5*/s32[]{:T(128)}, ...), condition=%wide.region_7.8_spmd, body=%wide.region_6.7_spmd.sunk | while | flops 981 | bytes 11843 | solution.py:27
  103.1 0.7 bitcast_add_fusion.5
  103.8 0.7 bitcast_add_fusion.5
  104.6 0.7 bitcast_add_fusion.5
  105.3 0.7 bitcast_add_fusion.5
  106.1 0.7 bitcast_add_fusion.5
  106.8 0.7 bitcast_add_fusion.5
  107.5 0.7 bitcast_add_fusion.5
  108.3 1.2 rev.7
  109.5 1.5 %fusion.36 = f32[3,64,13,25]{3,2,1,0:T(8,128)S(1)} fusion(f32[3,64,13,25]{3,2,1,0:T(8,128)} %rev.7), kind=kOutput, calls=%fused_computation.197 | output fusion | flops 3931200 | bytes 499200 | tf_op jit(solution)/shard_map/jit(cumsum)/reduce_window_sum | solution.py:131
  111.1 0.8 add_multiply_fusion
  111.9 0.8 copy.35
  112.7 2.2 %convolution_bitcast_fusion.1 = f32[3,64,32,25]{1,2,0,3:T(8,128)} fusion(f32[3,64,13,25]{1,2,0,3:T(8,128)S(1)} %copy.35, f32[32,13,25]{0,1,2:T(8,128)S(1)} %stack.74), kind=kOutput, calls=%fused_computation.4 | convolution fusion | flops 23961600 | bytes 905600 | tf_op jit(solution)/shard_map/frlk,tlk->frtk/dot_general | solution.py:139
  114.9 2.9 %copy.36 = f32[3,64,32,25]{3,2,1,0:T(8,128)S(1)} copy(f32[3,64,32,25]{1,2,0,3:T(8,128)} %convolution_bitcast_fusion.1) | data formatting | bytes 1228800 | tf_op jit(solution)/shard_map/frlk,tlk->frtk/transpose | solution.py:139
  117.8 13.2 %fusion.14 = f32[3,64,32,512]{3,2,1,0:T(8,128)} fusion(f32[3,64,32,25]{3,2,1,0:T(8,128)S(1)} %copy.36, f32[25]{0:T(128)S(1)} %fusion.29, f32[512]{0:T(512)S(1)} %iota_multiply_fusion, pred[25]{0:T(512)(128)(4,1)S(1)} %copy-done.2, pred[25]{0:T(512)(128)(4,1)S(1)} %copy-done.4), kind=kOutput, calls=%fused_computation.23 | convolution fusion | flops 943782400 | bytes 13199510 | tf_op jit(solution)/shard_map/dot_general | solution.py:140
  (62 shorter events, 1.7 us)
Async XLA Ops:
  6.5 69.3 %all-reduce.2.cloned.1.call-start = ((), (), s32[]{:S(2)}) async-start(), calls=%async_computation | async-start | bytes 360448 | tf_op jit(solution)/shard_map/psum | solution.py:116
  10.1 18.1 %copy-start.1 = (pred[25]{0:T(512)(128)(4,1)}, pred[25]{0:T(512)(128)(4,1)S(1)}, u32[]{:S(2)}) copy-start(pred[25]{0:T(512)(128)(4,1)S(1)} %get-tuple-element.109) | copy-start | bytes 79
  10.2 18.1 %copy-start.3 = (pred[25]{0:T(512)(128)(4,1)}, pred[25]{0:T(512)(128)(4,1)S(1)}, u32[]{:S(2)}) copy-start(pred[25]{0:T(512)(128)(4,1)S(1)} %get-tuple-element.110) | copy-start | bytes 79
  35.8 1.0 copy-start
  114.9 2.9 %copy-start.2 = (pred[25]{0:T(512)(128)(4,1)S(1)}, pred[25]{0:T(512)(128)(4,1)}, u32[]{:S(2)}) copy-start(pred[25]{0:T(512)(128)(4,1)} %copy-done.1) | copy-start | bytes 79
  114.9 2.9 %copy-start.4 = (pred[25]{0:T(512)(128)(4,1)S(1)}, pred[25]{0:T(512)(128)(4,1)}, u32[]{:S(2)}) copy-start(pred[25]{0:T(512)(128)(4,1)} %copy-done.3) | copy-start | bytes 79
Sparse Core Ops, SparseCore 0:
  38.4 37.3 all-reduce.1
where the time goes:
time: 139 us; the launch traced here: 138 us
  matrix products  39.5 us (28%)
  waiting for transfers between devices  37.2 us (27%)
  blocking collectives  24.5 us (18%)
  between operations  13.9 us (10%)
  other arithmetic  11.7 us (8%)
  local copies, waits for them, and re-layouts  11 us (8%)
    psum x1, waiting for transfers between devices, body(): summed = lax.psum(packed, 'ang')  37.2 us
    all_gather x2, blocking collectives, entering(): gathered = lax.all_gather(part, axis)  24.5 us
    dot_general x1, matrix products, body(): jnp.dot(density.reshape(snapshots * shells * theta_rows, phi_cells), four...  15.4 us
    dot_general x1, matrix products, body(): jnp.dot(spread.reshape(snapshots * shells * theta_rows, width), fourier.T...  13.2 us
    dot_general x1, matrix products, body(): jnp.einsum('frtk,tlk->frlk', azimuthal, legendre * weights[:, None, None]...  5.83 us
    add x7, other arithmetic, add_terms(): return jax.tree.map(jnp.add, earlier, later)  5.19 us
    transpose x1, local copies, waits for them, and re-layouts, body(): jnp.einsum('frlk,tlk->frtk', coefficient, legendre, precision=lax.Precisi...  2.88 us
  transfers between devices with their start and end apart: 1, of which 1 were waited for; matrix products, arithmetic and copies ran while one was open for 0% of the time, Pallas kernels for 0%

commit v1 on v0

v1 whole, which is shorter than its diff:
```python
import functools
import math

import jax
import jax.numpy as jnp
import numpy as np
from jax import lax
from jax.experimental import pallas as pl
from jax.experimental.pallas import tpu as pltpu
from jax.sharding import PartitionSpec as P

LMAX = 12
INNER = 0.5
COUPLING = 2000.0
LANES = 128
MESH = pl.DeviceIdType.MESH
SLOTS = [(l, k) for l in range(LMAX + 1) for k in range(2 * LMAX + 1) if (k + 1) // 2 <= l]
EVEN = [s for s in SLOTS if ((s[1] + 1) // 2) % 2 == 0]
ODD = [s for s in SLOTS if ((s[1] + 1) // 2) % 2 == 1]


def legendre_rows(total_rows):
    angle = (np.arange(total_rows) + 0.5) * (math.pi / total_rows)
    c, s = np.cos(angle), np.sin(angle)
    v = {(0, 0): np.full_like(angle, 1.0 / math.sqrt(4.0 * math.pi))}
    for m in range(1, LMAX + 1):
        v[m, m] = math.sqrt((2.0 * m + 1.0) / (2.0 * m)) * s * v[m - 1, m - 1]
    for m in range(LMAX):
        v[m + 1, m] = math.sqrt(2.0 * m + 3.0) * c * v[m, m]
    for m in range(LMAX + 1):
        for l in range(m + 2, LMAX + 1):
            a = math.sqrt((4.0 * l * l - 1.0) / (l * l - m * m))
            b = math.sqrt(((l - 1.0) ** 2 - m * m) / (4.0 * (l - 1.0) ** 2 - 1.0))
            v[l, m] = a * (c * v[l - 1, m] - b * v[l - 2, m])
    table = np.zeros((total_rows, 2 * LANES))
    for base, group in ((0, EVEN), (LANES, ODD)):
        for n, (l, k) in enumerate(group):
            table[:, base + n] = v[l, (k + 1) // 2]
    return table, s


def fourier_columns(phi_cells, group):
    phi = np.arange(phi_cells // 2) * (2.0 * math.pi / phi_cells)
    table = np.zeros((phi_cells // 2, LANES))
    for n, (_, k) in enumerate(group):
        m = (k + 1) // 2
        if k == 0:
            table[:, n] = 1.0
        else:
            table[:, n] = math.sqrt(2.0) * (np.cos(m * phi) if k % 2 else np.sin(m * phi))
    return table


def split_np(table):
    hi = np.asarray(table, np.float32).astype(jnp.bfloat16)
    lo = (table - hi.astype(np.float64)).astype(np.float32).astype(jnp.bfloat16)
    return hi, lo


def split(x):
    hi = x.astype(jnp.bfloat16)
    return hi, (x - hi.astype(jnp.float32)).astype(jnp.bfloat16)


class Packing:
    def __init__(self, owners, fields):
        half = owners // 2
        main = len(ODD)
        self.piece = -(-main // half)
        assert fields * self.piece <= LANES - 2 and fields <= owners
        self.moves = []
        for parity, count, base in ((0, half, 0), (1, owners - half, half)):
            for n in range(count):
                start = n * self.piece
                size = min(self.piece, main - start)
                if size > 0:
                    self.moves.append((base + n, parity, start, size))
        self.owners, self.fields = owners, fields
        self.last = len(EVEN) - 1
        self.spare = LANES - 2

    def degrees(self):
        table = np.zeros((-(-self.owners // 8) * 8, LANES), np.float32)
        for f in range(self.fields):
            for q, parity, start, size in self.moves:
                group = (EVEN, ODD)[parity]
                for n in range(size):
                    table[q, f * self.piece + n] = group[start + n][0]
            table[f, self.spare] = EVEN[self.last][0]
        return table

    def pack(self, tiles):
        lane = lax.broadcasted_iota(jnp.int32, tiles[0][0].shape, 1)
        out = [jnp.zeros_like(tiles[0][0]) for _ in range(self.owners)]
        for f in range(self.fields):
            for q, parity, start, size in self.moves:
                to = f * self.piece
                moved = pltpu.roll(tiles[f][parity], (to - start) % LANES, 1)
                out[q] = jnp.where((lane >= to) & (lane < to + size), moved, out[q])
            moved = pltpu.roll(tiles[f][0], (self.spare - self.last) % LANES, 1)
            out[f] = jnp.where(lane == self.spare, moved, out[f])
        return out

    def unpack(self, packed, f):
        lane = lax.broadcasted_iota(jnp.int32, packed[0].shape, 1)
        out = [jnp.zeros_like(packed[0]) for _ in range(2)]
        for q, parity, start, size in self.moves:
            moved = pltpu.roll(packed[q], (start - f * self.piece) % LANES, 1)
            out[parity] = jnp.where((lane >= start) & (lane < start + size), moved, out[parity])
        moved = pltpu.roll(packed[f], (self.last - self.spare) % LANES, 1)
        out[0] = jnp.where(lane == self.last, moved, out[0])
        return out


def moments_kernel(
    n_rad, n_ang, packing, group, density, even_w, odd_w, weighted, degrees, out,
    rows_buf, even_buf, odd_buf, leg_buf, part, landed, totals, totals_in, coef,
    load_sem, table_sem, part_send, part_recv, tot_send, tot_recv, coef_send, coef_recv,
):
    fields, shells, thetas, phis = density.shape
    groups = shells // group
    half = phis // 2
    rad, ang = lax.axis_index("rad"), lax.axis_index("ang")

    def load(g, f):
        return pltpu.make_async_copy(
            density.at[f, pl.ds(g * group, group)], rows_buf.at[g * fields + f],
            load_sem.at[g * fields + f],
        )

    tables = [
        pltpu.make_async_copy(even_w, even_buf, table_sem.at[0]),
        pltpu.make_async_copy(odd_w, odd_buf, table_sem.at[1]),
        pltpu.make_async_copy(weighted.at[pl.ds(ang * thetas, thetas)], leg_buf, table_sem.at[2]),
    ]
    for copy in tables:
        copy.start()
    for g in range(groups):
        for f in range(fields):
            load(g, f).start()

    barrier = pltpu.get_barrier_semaphore()
    for d in range(1, n_ang):
        pl.semaphore_signal(
            barrier, inc=1, device_id=(rad, lax.rem(ang + d, n_ang)), device_id_type=MESH
        )
    for d in range(1, n_rad):
        pl.semaphore_signal(
            barrier, inc=1, device_id=(lax.rem(rad + d, n_rad), ang), device_id_type=MESH
        )

    def send_part(g, d):
        q = lax.rem(ang + d, n_ang)
        at = pl.ds(pl.multiple_of(g * group, group), group)
        return pltpu.make_async_remote_copy(
            src_ref=part.at[q, at], dst_ref=landed.at[n_ang - 1 - d, at],
            send_sem=part_send.at[d - 1, g], recv_sem=part_recv.at[n_ang - 1 - d, g],
            device_id=(rad, q), device_id_type=MESH,
        )

    def recv_part(g, slot):
        at = pl.ds(pl.multiple_of(g * group, group), group)
        return pltpu.make_async_remote_copy(
            src_ref=part.at[0, at], dst_ref=landed.at[slot, at],
            send_sem=part_send.at[slot, g], recv_sem=part_recv.at[slot, g],
            device_id=(rad, lax.rem(ang + 1, n_ang)), device_id_type=MESH,
        )

    degree = degrees[pl.ds(ang, 1), :]
    total_shells = shells * n_rad
    spacing = (1.0 - INNER) / total_shells
    index = rad * shells + lax.broadcasted_iota(jnp.int32, (shells, LANES), 0)
    log_r = jnp.log(INNER + (index.astype(jnp.float32) + 0.5) * spacing)
    factor = (-COUPLING * 4.0 * math.pi) / (2.0 * degree + 1.0)
    inner_w = jnp.exp((degree + 2.0) * log_r) * spacing
    outer_w = jnp.exp((1.0 - degree) * log_r) * spacing
    inner_c = factor * jnp.exp(-(degree + 1.0) * log_r)
    outer_c = factor * jnp.exp(degree * log_r)

    for copy in tables:
        copy.wait()

    def one(g, _):
        tiles = []
        for f in range(fields):
            load(g, f).wait()
            x = rows_buf[g * fields + f].reshape(group * thetas, phis)
            left, right = x[:, :half], x[:, half:]
            pair = []
            for n, (v, w) in enumerate(((left + right, even_buf), (left - right, odd_buf))):
                hi, lo = split(v)
                both = jnp.dot(hi, w[...], preferred_element_type=jnp.float32)
                rest = jnp.dot(lo, w[:, :LANES], preferred_element_type=jnp.float32)
                az = both[:, :LANES] + both[:, LANES:] + rest
                az = az.reshape(group, thetas, LANES)
                az = az * leg_buf[:, n * LANES:(n + 1) * LANES][None]
                pair.append(jnp.sum(az, axis=1))
            tiles.append(pair)
        packed = packing.pack(tiles)
        at = pl.ds(pl.multiple_of(g * group, group), group)
        for q in range(n_ang):
            part[q, at, :] = packed[q]

        @pl.when(g == 0)
        def _():
            pl.semaphore_wait(barrier, n_ang + n_rad - 2)

        for d in range(1, n_ang):
            send_part(g, d).start()
        return 0

    lax.fori_loop(0, groups, one, 0)

    for g in range(groups):
        for slot in range(n_ang - 1):
            recv_part(g, slot).wait_recv()
    moments = part[ang]
    for slot in range(n_ang - 1):
        moments = moments + landed[slot]
    inner = moments * inner_w
    outer = moments * outer_w
    sub = lax.broadcasted_iota(jnp.int32, (8, LANES), 0)
    inner_total = jnp.sum(inner, axis=0, keepdims=True)
    outer_total = jnp.sum(outer, axis=0, keepdims=True)
    totals[...] = jnp.where(sub == 0, inner_total, jnp.where(sub == 1, outer_total, 0.0))

    def send_total(d):
        slot = n_rad - 1 - d
        return pltpu.make_async_remote_copy(
            src_ref=totals, dst_ref=totals_in.at[slot],
            send_sem=tot_send.at[d - 1], recv_sem=tot_recv.at[slot],
            device_id=(lax.rem(rad + d, n_rad), ang), device_id_type=MESH,
        )

    for d in range(1, n_rad):
        send_total(d).start()

    row = lax.broadcasted_iota(jnp.int32, (shells, shells), 0)
    col = lax.broadcasted_iota(jnp.int32, (shells, shells), 1)
    diag = jnp.where(row == col, 0.5, 0.0)
    below = jnp.where(col < row, 1.0, diag)
    above = jnp.where(col > row, 1.0, diag)
    inner_sum = jnp.dot(below, inner, precision=lax.Precision.HIGHEST, preferred_element_type=jnp.float32)
    outer_sum = jnp.dot(above, outer, precision=lax.Precision.HIGHEST, preferred_element_type=jnp.float32)

    from_below = jnp.zeros((1, LANES), jnp.float32)
    from_above = jnp.zeros((1, LANES), jnp.float32)
    for slot in range(n_rad - 1):
        send_total(n_rad - 1 - slot).wait_recv()
        source = lax.rem(rad + slot + 1, n_rad)
        got = totals_in[slot]
        from_below = from_below + jnp.where(source < rad, got[0:1], 0.0)
        from_above = from_above + jnp.where(source > rad, got[1:2], 0.0)
    coef[ang] = inner_c * (from_below + inner_sum) + outer_c * (from_above + outer_sum)

    def send_coef(d):
        return pltpu.make_async_remote_copy(
            src_ref=coef.at[ang], dst_ref=coef.at[ang],
            send_sem=coef_send.at[d - 1], recv_sem=coef_recv.at[n_ang - 1 - d],
            device_id=(rad, lax.rem(ang + d, n_ang)), device_id_type=MESH,
        )

    def recv_coef(d):
        q = lax.rem(ang + n_ang - d, n_ang)
        return pltpu.make_async_remote_copy(
            src_ref=coef.at[ang], dst_ref=coef.at[q],
            send_sem=coef_send.at[d - 1], recv_sem=coef_recv.at[n_ang - 1 - d],
            device_id=(rad, q), device_id_type=MESH,
        )

    for d in range(1, n_ang):
        send_coef(d).start()
    for d in range(1, n_ang):
        recv_coef(d).wait_recv()
    out[...] = coef[...]
    for d in range(1, n_ang):
        send_coef(d).wait_send()
        for g in range(groups):
            send_part(g, d).wait_send()
    for d in range(1, n_rad):
        send_total(d).wait_send()


def potential_kernel(packing, group, coef, legendre, even_w, odd_w, out, spread, rows_buf, store_sem):
    fields, shells, thetas, phis = out.shape
    groups = shells // group
    half = phis // 2
    first = pl.multiple_of(lax.axis_index("ang") * thetas, thetas)
    tiles = [coef[q] for q in range(packing.owners)]
    for f in range(fields):
        for parity, value in enumerate(packing.unpack(tiles, f)):
            spread[f, :, parity * LANES:(parity + 1) * LANES] = value

    def store(c):
        f, g = c // groups, c % groups
        return pltpu.make_async_copy(
            rows_buf.at[c], out.at[f, pl.ds(g * group, group)], store_sem.at[c]
        )

    def one(c, _):
        f, g = c // groups, c % groups
        sides = []
        for n, w in enumerate((even_w, odd_w)):
            lanes = slice(n * LANES, (n + 1) * LANES)
            c_rows = spread[f, pl.ds(pl.multiple_of(g * group, group), group), lanes]
            s = c_rows[:, None, :] * legendre[pl.ds(first, thetas), lanes][None]
            hi, lo = split(s.reshape(group * thetas, LANES))
            main = jnp.dot(
                jnp.concatenate([hi, lo], 1), w[: 2 * LANES], preferred_element_type=jnp.float32
            )
            rest = jnp.dot(hi, w[2 * LANES:], preferred_element_type=jnp.float32)
            sides.append(main + rest)
        rows_buf[c, :, :, :half] = (sides[0] + sides[1]).reshape(group, thetas, half)
        rows_buf[c, :, :, half:] = (sides[0] - sides[1]).reshape(group, thetas, half)
        store(c).start()
        return 0

    lax.fori_loop(0, fields * groups, one, 0)
    for c in range(fields * groups):
        store(c).wait()


def body(n_rad, n_ang, density):
    fields, shells, thetas, phis = density.shape
    group = math.gcd(shells, 16)
    groups = shells // group
    packing = Packing(n_ang, fields)
    total_rows = thetas * n_ang
    legendre, sine = legendre_rows(total_rows)
    weights = sine * (math.pi / total_rows) * (2.0 * math.pi / phis)
    weighted = jnp.asarray(legendre * weights[:, None], jnp.float32)
    forward, inverse = [], []
    for slots in (EVEN, ODD):
        table = fourier_columns(phis, slots)
        hi, lo = split_np(table)
        forward.append(jnp.asarray(np.concatenate([hi, lo], 1)))
        inverse.append(jnp.asarray(np.concatenate([hi.T, hi.T, lo.T], 0)))
    vmem = pl.BlockSpec(memory_space=pltpu.VMEM)
    anywhere = pl.BlockSpec(memory_space=pl.ANY)
    dma = pltpu.SemaphoreType.DMA
    coef = pl.pallas_call(
        functools.partial(moments_kernel, n_rad, n_ang, packing, group),
        out_shape=jax.ShapeDtypeStruct((n_ang, shells, LANES), jnp.float32),
        in_specs=[anywhere] * 4 + [vmem],
        out_specs=vmem,
        scratch_shapes=[
            pltpu.VMEM((fields * groups, group, thetas, phis), jnp.float32),
            pltpu.VMEM((phis // 2, 2 * LANES), jnp.bfloat16),
            pltpu.VMEM((phis // 2, 2 * LANES), jnp.bfloat16),
            pltpu.VMEM((thetas, 2 * LANES), jnp.float32),
            pltpu.VMEM((n_ang, shells, LANES), jnp.float32),
            pltpu.VMEM((n_ang - 1, shells, LANES), jnp.float32),
            pltpu.VMEM((8, LANES), jnp.float32),
            pltpu.VMEM((n_rad - 1, 8, LANES), jnp.float32),
            pltpu.VMEM((n_ang, shells, LANES), jnp.float32),
            dma((fields * groups,)),
            dma((3,)),
            dma((n_ang - 1, groups)),
            dma((n_ang - 1, groups)),
            dma((n_rad - 1,)),
            dma((n_rad - 1,)),
            dma((n_ang - 1,)),
            dma((n_ang - 1,)),
        ],
        compiler_params=pltpu.CompilerParams(collective_id=0, has_side_effects=True),
        name="moments",
    )(density, forward[0], forward[1], weighted, jnp.asarray(packing.degrees()))
    return pl.pallas_call(
        functools.partial(potential_kernel, packing, group),
        out_shape=jax.ShapeDtypeStruct(density.shape, jnp.float32),
        in_specs=[vmem] * 4,
        out_specs=anywhere,
        scratch_shapes=[
            pltpu.VMEM((fields, shells, 2 * LANES), jnp.float32),
            pltpu.VMEM((fields * groups, group, thetas, phis), jnp.float32),
            dma((fields * groups,)),
        ],
        name="potential",
    )(coef, jnp.asarray(legendre, jnp.float32), inverse[0], inverse[1])


def solution(mesh):
    sizes = mesh.shape
    return jax.shard_map(
        functools.partial(body, sizes["rad"], sizes["ang"]),
        mesh=mesh,
        in_specs=(P(None, "rad", "ang", None),),
        out_specs=P(None, "rad", "ang", None),
        check_vma=False,
    )
```

time: 139 us -> 34 us (0.24)
  matrix products: 39.5 us -> 0 us
  waiting for transfers between devices: 37.2 us -> 0 us
  Pallas kernels: 0 us -> 33.8 us
  blocking collectives: 24.5 us -> 0 us
  between operations: 13.9 us -> 0.01 us
  other arithmetic: 11.7 us -> 0 us
  local copies, waits for them, and re-layouts: 11 us -> 0 us
    dot_general x6 -> x0, matrix products: 39.5 us -> none  [the longest x1 15.4 us: body(): jnp.dot(density.reshape(snapshots * shells * theta_rows, phi_cells), four...]
    psum x1 -> x0, waiting for transfers between devices: 37.2 us -> none  [body(): summed = lax.psum(packed, 'ang')]
    pallas_call x0 -> x2, Pallas kernels: none -> 33.8 us  [the longest x1 26.3 us: body(): pl.pallas_call(functools.partial(moments_kernel, n_rad, n_ang, packing, g...]
    all_gather x2 -> x0, blocking collectives: 24.5 us -> none  [entering(): gathered = lax.all_gather(part, axis)]
    add x8 -> x0, other arithmetic: 5.2 us -> none  [the longest x7 5.19 us: add_terms(): return jax.tree.map(jnp.add, earlier, later)]
    mul x47 -> x0, other arithmetic: 3.44 us -> none  [the longest x33 2.22 us: legendre_table(): coef_a * (cos_theta * values_lm[l - 1, m] - coef_b * values_lm[l - 2, m])]
    another operation x29 -> x0, local copies, waits for them, and re-layouts: 3.41 us -> none  [the longest x12 2.28 us: legendre_table(): degree_rows.append(jnp.stack(columns, -1))]
    transpose x2 -> x0, local copies, waits for them, and re-layouts: 3.14 us -> none  [the longest x1 2.88 us: body(): jnp.einsum('frlk,tlk->frtk', coefficient, legendre, precision=lax.Precisi...]
  transfers between devices with their start and end apart: 1 -> 0, of which waited for: 1 -> 0; matrix products, arithmetic and copies ran while one was open for 0% -> 0% of each run, Pallas kernels for 0% -> 0%
where the time goes in v1:
time: 34 us; the launch traced here: 33.8 us
  Pallas kernels  33.8 us (99%)
    pallas_call x1, Pallas kernels, body(): pl.pallas_call(functools.partial(moments_kernel, n_rad, n_ang, packing, g...  26.3 us
    pallas_call x1, Pallas kernels, body(): pl.pallas_call(functools.partial(potential_kernel, packing, group), out_s...  7.45 us

profile of v1, /device:TPU:0, one launch (start us, length us, event | category | flops | bytes accessed | tf_op | source)
XLA Modules:
  0.0 33.8 jit_solution(2314909681563738370)
XLA Ops:
  0.0 26.3 %moments.1.coef = f32[4,64,128]{2,1,0:T(8,128)} custom-call(f32[3,64,32,512]{3,2,1,0:T(8,128)} %density.1, bf16[256,256]{1,0:T(8,128)(2,1)} %constant.15.clone.even_w, bf16[256,256]{1,0:T(8,128)(2,1)} %constant.17.clone.odd_w, f32[128,256]{1,0:T(8,128)} %constant.14.clone.weighted, f32[8,128]{1,0:T(8,128)} %constant.19.clone.degrees), custom_call_target="tpu_custom_call" | custom-call | tf_op jit(solution)/shard_map/moments/pallas_call | solution.py:341
  26.3 7.5 %potential.1 = f32[3,64,32,512]{3,2,1,0:T(8,128)} custom-call(f32[4,64,128]{2,1,0:T(8,128)} %moments.1.coef, f32[128,256]{1,0:T(8,128)} %constant.20.clone.legendre, bf16[384,256]{1,0:T(8,128)(2,1)} %constant.16.clone.even_w, bf16[384,256]{1,0:T(8,128)(2,1)} %constant.18.clone.odd_w), custom_call_target="tpu_custom_call" | custom-call | tf_op jit(solution)/shard_map/potential/pallas_call | solution.py:368

commit v2 on v1

--- a/solution.py
+++ b/solution.py
@@ -114,7 +114,7 @@
 
 def moments_kernel(
     n_rad, n_ang, packing, group, density, even_w, odd_w, weighted, degrees, out,
-    rows_buf, even_buf, odd_buf, leg_buf, part, landed, totals, totals_in, coef,
+    rows_buf, even_buf, odd_buf, leg_buf, part, landed, totals, totals_in, coef, powers,
     load_sem, table_sem, part_send, part_recv, tot_send, tot_recv, coef_send, coef_recv,
 ):
     fields, shells, thetas, phis = density.shape
@@ -135,9 +135,9 @@
     ]
     for copy in tables:
         copy.start()
-    for g in range(groups):
-        for f in range(fields):
-            load(g, f).start()
+    ahead = min(2, groups * fields)
+    for c in range(ahead):
+        load(c // fields, c % fields).start()
 
     barrier = pltpu.get_barrier_semaphore()
     for d in range(1, n_ang):
@@ -145,9 +145,11 @@
             barrier, inc=1, device_id=(rad, lax.rem(ang + d, n_ang)), device_id_type=MESH
         )
     for d in range(1, n_rad):
-        pl.semaphore_signal(
-            barrier, inc=1, device_id=(lax.rem(rad + d, n_rad), ang), device_id_type=MESH
-        )
+        for z in range(n_ang):
+            pl.semaphore_signal(
+                barrier, inc=1, device_id=(lax.rem(rad + d, n_rad), lax.rem(ang + z, n_ang)),
+                device_id_type=MESH,
+            )
 
     def send_part(g, d):
         q = lax.rem(ang + d, n_ang)
@@ -172,8 +174,9 @@
     index = rad * shells + lax.broadcasted_iota(jnp.int32, (shells, LANES), 0)
     log_r = jnp.log(INNER + (index.astype(jnp.float32) + 0.5) * spacing)
     factor = (-COUPLING * 4.0 * math.pi) / (2.0 * degree + 1.0)
-    inner_w = jnp.exp((degree + 2.0) * log_r) * spacing
-    outer_w = jnp.exp((1.0 - degree) * log_r) * spacing
+    for q in range(n_ang):
+        powers[0, q] = jnp.exp((degrees[q:q + 1, :] + 2.0) * log_r) * spacing
+        powers[1, q] = jnp.exp((1.0 - degrees[q:q + 1, :]) * log_r) * spacing
     inner_c = factor * jnp.exp(-(degree + 1.0) * log_r)
     outer_c = factor * jnp.exp(degree * log_r)
 
@@ -184,6 +187,12 @@
         tiles = []
         for f in range(fields):
             load(g, f).wait()
+            c = g * fields + f + ahead
+
+            @pl.when(c < groups * fields)
+            def _():
+                load(c // fields, c % fields).start()
+
             x = rows_buf[g * fields + f].reshape(group * thetas, phis)
             left, right = x[:, :half], x[:, half:]
             pair = []
@@ -203,13 +212,32 @@
 
         @pl.when(g == 0)
         def _():
-            pl.semaphore_wait(barrier, n_ang + n_rad - 2)
+            pl.semaphore_wait(barrier, n_ang * n_rad - 1)
 
         for d in range(1, n_ang):
             send_part(g, d).start()
         return 0
 
     lax.fori_loop(0, groups, one, 0)
+
+    sub = lax.broadcasted_iota(jnp.int32, (8, LANES), 0)
+    for q in range(n_ang):
+        inner_total = jnp.sum(part[q] * powers[0, q], axis=0, keepdims=True)
+        outer_total = jnp.sum(part[q] * powers[1, q], axis=0, keepdims=True)
+        totals[q] = jnp.where(sub == 0, inner_total, jnp.where(sub == 1, outer_total, 0.0))
+
+    def send_total(d, z):
+        slot = n_rad - 1 - d
+        q = lax.rem(ang + z, n_ang)
+        return pltpu.make_async_remote_copy(
+            src_ref=totals.at[q], dst_ref=totals_in.at[slot, z],
+            send_sem=tot_send.at[d - 1, z], recv_sem=tot_recv.at[slot, z],
+            device_id=(lax.rem(rad + d, n_rad), q), device_id_type=MESH,
+        )
+
+    for z in [*range(1, n_ang), 0]:
+        for d in range(1, n_rad):
+            send_total(d, z).start()
 
     for g in range(groups):
         for slot in range(n_ang - 1):
@@ -217,24 +245,8 @@
     moments = part[ang]
     for slot in range(n_ang - 1):
         moments = moments + landed[slot]
-    inner = moments * inner_w
-    outer = moments * outer_w
-    sub = lax.broadcasted_iota(jnp.int32, (8, LANES), 0)
-    inner_total = jnp.sum(inner, axis=0, keepdims=True)
-    outer_total = jnp.sum(outer, axis=0, keepdims=True)
-    totals[...] = jnp.where(sub == 0, inner_total, jnp.where(sub == 1, outer_total, 0.0))
-
-    def send_total(d):
-        slot = n_rad - 1 - d
-        return pltpu.make_async_remote_copy(
-            src_ref=totals, dst_ref=totals_in.at[slot],
-            send_sem=tot_send.at[d - 1], recv_sem=tot_recv.at[slot],
-            device_id=(lax.rem(rad + d, n_rad), ang), device_id_type=MESH,
-        )
-
-    for d in range(1, n_rad):
-        send_total(d).start()
-
+    inner = moments * powers[0, ang]
+    outer = moments * powers[1, ang]
     row = lax.broadcasted_iota(jnp.int32, (shells, shells), 0)
     col = lax.broadcasted_iota(jnp.int32, (shells, shells), 1)
     diag = jnp.where(row == col, 0.5, 0.0)
@@ -243,15 +255,19 @@
     inner_sum = jnp.dot(below, inner, precision=lax.Precision.HIGHEST, preferred_element_type=jnp.float32)
     outer_sum = jnp.dot(above, outer, precision=lax.Precision.HIGHEST, preferred_element_type=jnp.float32)
 
-    from_below = jnp.zeros((1, LANES), jnp.float32)
-    from_above = jnp.zeros((1, LANES), jnp.float32)
+    from_below = jnp.zeros((8, LANES), jnp.float32)
+    from_above = jnp.zeros((8, LANES), jnp.float32)
     for slot in range(n_rad - 1):
-        send_total(n_rad - 1 - slot).wait_recv()
+        got = jnp.zeros((8, LANES), jnp.float32)
+        for z in range(n_ang):
+            send_total(n_rad - 1 - slot, z).wait_recv()
+            got = got + totals_in[slot, z]
         source = lax.rem(rad + slot + 1, n_rad)
-        got = totals_in[slot]
-        from_below = from_below + jnp.where(source < rad, got[0:1], 0.0)
-        from_above = from_above + jnp.where(source > rad, got[1:2], 0.0)
-    coef[ang] = inner_c * (from_below + inner_sum) + outer_c * (from_above + outer_sum)
+        from_below = from_below + jnp.where(source < rad, got, 0.0)
+        from_above = from_above + jnp.where(source > rad, got, 0.0)
+    coef[ang] = inner_c * (from_below[0:1] + inner_sum) + outer_c * (
+        from_above[1:2] + outer_sum
+    )
 
     def send_coef(d):
         return pltpu.make_async_remote_copy(
@@ -278,7 +294,8 @@
         for g in range(groups):
             send_part(g, d).wait_send()
     for d in range(1, n_rad):
-        send_total(d).wait_send()
+        for z in range(n_ang):
+            send_total(d, z).wait_send()
 
 
 def potential_kernel(packing, group, coef, legendre, even_w, odd_w, out, spread, rows_buf, store_sem):
@@ -322,7 +339,7 @@
 
 def body(n_rad, n_ang, density):
     fields, shells, thetas, phis = density.shape
-    group = math.gcd(shells, 16)
+    group = math.gcd(shells, 32)
     groups = shells // group
     packing = Packing(n_ang, fields)
     total_rows = thetas * n_ang
@@ -350,15 +367,16 @@
             pltpu.VMEM((thetas, 2 * LANES), jnp.float32),
             pltpu.VMEM((n_ang, shells, LANES), jnp.float32),
             pltpu.VMEM((n_ang - 1, shells, LANES), jnp.float32),
-            pltpu.VMEM((8, LANES), jnp.float32),
-            pltpu.VMEM((n_rad - 1, 8, LANES), jnp.float32),
+            pltpu.VMEM((n_ang, 8, LANES), jnp.float32),
+            pltpu.VMEM((n_rad - 1, n_ang, 8, LANES), jnp.float32),
             pltpu.VMEM((n_ang, shells, LANES), jnp.float32),
+            pltpu.VMEM((2, n_ang, shells, LANES), jnp.float32),
             dma((fields * groups,)),
             dma((3,)),
             dma((n_ang - 1, groups)),
             dma((n_ang - 1, groups)),
-            dma((n_rad - 1,)),
-            dma((n_rad - 1,)),
+            dma((n_rad - 1, n_ang)),
+            dma((n_rad - 1, n_ang)),
             dma((n_ang - 1,)),
             dma((n_ang - 1,)),
         ],

time: 34 us -> 30.5 us (0.90)
  Pallas kernels: 33.8 us -> 30.3 us
    pallas_call x1, Pallas kernels: 26.3 us -> 23.4 us  [body(): pl.pallas_call(functools.partial(moments_kernel, n_rad, n_ang, packing, g...]
    pallas_call x1, Pallas kernels: 7.45 us -> 6.86 us  [body(): pl.pallas_call(functools.partial(potential_kernel, packing, group), out_s...]
where the time goes in v2:
time: 30.5 us; the launch traced here: 30.3 us
  Pallas kernels  30.3 us (99%)
    pallas_call x1, Pallas kernels, body(): pl.pallas_call(functools.partial(moments_kernel, n_rad, n_ang, packing, g...  23.4 us
    pallas_call x1, Pallas kernels, body(): pl.pallas_call(functools.partial(potential_kernel, packing, group), out_s...  6.86 us

profile of v2, /device:TPU:0, one launch (start us, length us, event | category | flops | bytes accessed | tf_op | source)
XLA Modules:
  0.0 30.3 jit_solution(7178969888782411047)
XLA Ops:
  0.0 23.4 %moments.1.coef = f32[4,64,128]{2,1,0:T(8,128)} custom-call(f32[3,64,32,512]{3,2,1,0:T(8,128)} %density.1, bf16[256,256]{1,0:T(8,128)(2,1)} %constant.15.clone.even_w, bf16[256,256]{1,0:T(8,128)(2,1)} %constant.17.clone.odd_w, f32[128,256]{1,0:T(8,128)} %constant.14.clone.weighted, f32[8,128]{1,0:T(8,128)} %constant.19.clone.degrees), custom_call_target="tpu_custom_call" | custom-call | tf_op jit(solution)/shard_map/moments/pallas_call | solution.py:358
  23.4 6.9 %potential.1 = f32[3,64,32,512]{3,2,1,0:T(8,128)} custom-call(f32[4,64,128]{2,1,0:T(8,128)} %moments.1.coef, f32[128,256]{1,0:T(8,128)} %constant.20.clone.legendre, bf16[384,256]{1,0:T(8,128)(2,1)} %constant.16.clone.even_w, bf16[384,256]{1,0:T(8,128)(2,1)} %constant.18.clone.odd_w), custom_call_target="tpu_custom_call" | custom-call | tf_op jit(solution)/shard_map/potential/pallas_call | solution.py:386

commit v3 on v2

--- a/solution.py
+++ b/solution.py
@@ -113,9 +113,9 @@
 
 
 def moments_kernel(
-    n_rad, n_ang, packing, group, density, even_w, odd_w, weighted, degrees, out,
-    rows_buf, even_buf, odd_buf, leg_buf, part, landed, totals, totals_in, coef, powers,
-    load_sem, table_sem, part_send, part_recv, tot_send, tot_recv, coef_send, coef_recv,
+    n_rad, n_ang, packing, group, density, table, out,
+    rows_buf, even_buf, odd_buf, part, landed, totals, totals_in, coef, powers,
+    load_sem, part_send, part_recv, tot_send, tot_recv, coef_send, coef_recv,
 ):
     fields, shells, thetas, phis = density.shape
     groups = shells // group
@@ -128,13 +128,6 @@
             load_sem.at[g * fields + f],
         )
 
-    tables = [
-        pltpu.make_async_copy(even_w, even_buf, table_sem.at[0]),
-        pltpu.make_async_copy(odd_w, odd_buf, table_sem.at[1]),
-        pltpu.make_async_copy(weighted.at[pl.ds(ang * thetas, thetas)], leg_buf, table_sem.at[2]),
-    ]
-    for copy in tables:
-        copy.start()
     ahead = min(2, groups * fields)
     for c in range(ahead):
         load(c // fields, c % fields).start()
@@ -168,7 +161,11 @@
             device_id=(rad, lax.rem(ang + 1, n_ang)), device_id_type=MESH,
         )
 
-    degree = degrees[pl.ds(ang, 1), :]
+    degrees = table[phis + n_ang * thetas:, :LANES]
+
+    degree = degrees[0:1]
+    for q in range(1, n_ang):
+        degree = jnp.where(ang == q, degrees[q:q + 1], degree)
     total_shells = shells * n_rad
     spacing = (1.0 - INNER) / total_shells
     index = rad * shells + lax.broadcasted_iota(jnp.int32, (shells, LANES), 0)
@@ -180,8 +177,9 @@
     inner_c = factor * jnp.exp(-(degree + 1.0) * log_r)
     outer_c = factor * jnp.exp(degree * log_r)
 
-    for copy in tables:
-        copy.wait()
+    even_buf[...] = table[:half].astype(jnp.bfloat16)
+    odd_buf[...] = table[half:phis].astype(jnp.bfloat16)
+    leg_at = pl.ds(pl.multiple_of(phis + ang * thetas, thetas), thetas)
 
     def one(g, _):
         tiles = []
@@ -202,7 +200,7 @@
                 rest = jnp.dot(lo, w[:, :LANES], preferred_element_type=jnp.float32)
                 az = both[:, :LANES] + both[:, LANES:] + rest
                 az = az.reshape(group, thetas, LANES)
-                az = az * leg_buf[:, n * LANES:(n + 1) * LANES][None]
+                az = az * table[leg_at, n * LANES:(n + 1) * LANES][None]
                 pair.append(jnp.sum(az, axis=1))
             tiles.append(pair)
         packed = packing.pack(tiles)
@@ -345,26 +343,27 @@
     total_rows = thetas * n_ang
     legendre, sine = legendre_rows(total_rows)
     weights = sine * (math.pi / total_rows) * (2.0 * math.pi / phis)
-    weighted = jnp.asarray(legendre * weights[:, None], jnp.float32)
+    weighted = np.asarray(legendre * weights[:, None], np.float32)
     forward, inverse = [], []
     for slots in (EVEN, ODD):
         table = fourier_columns(phis, slots)
         hi, lo = split_np(table)
-        forward.append(jnp.asarray(np.concatenate([hi, lo], 1)))
+        forward.append(np.concatenate([hi, lo], 1).astype(np.float32))
         inverse.append(jnp.asarray(np.concatenate([hi.T, hi.T, lo.T], 0)))
+    degrees = np.tile(packing.degrees(), (1, 2))
+    table = jnp.asarray(np.concatenate([*forward, weighted, degrees], 0))
     vmem = pl.BlockSpec(memory_space=pltpu.VMEM)
     anywhere = pl.BlockSpec(memory_space=pl.ANY)
     dma = pltpu.SemaphoreType.DMA
     coef = pl.pallas_call(
         functools.partial(moments_kernel, n_rad, n_ang, packing, group),
         out_shape=jax.ShapeDtypeStruct((n_ang, shells, LANES), jnp.float32),
-        in_specs=[anywhere] * 4 + [vmem],
+        in_specs=[anywhere, vmem],
         out_specs=vmem,
         scratch_shapes=[
             pltpu.VMEM((fields * groups, group, thetas, phis), jnp.float32),
             pltpu.VMEM((phis // 2, 2 * LANES), jnp.bfloat16),
             pltpu.VMEM((phis // 2, 2 * LANES), jnp.bfloat16),
-            pltpu.VMEM((thetas, 2 * LANES), jnp.float32),
             pltpu.VMEM((n_ang, shells, LANES), jnp.float32),
             pltpu.VMEM((n_ang - 1, shells, LANES), jnp.float32),
             pltpu.VMEM((n_ang, 8, LANES), jnp.float32),
@@ -372,7 +371,6 @@
             pltpu.VMEM((n_ang, shells, LANES), jnp.float32),
             pltpu.VMEM((2, n_ang, shells, LANES), jnp.float32),
             dma((fields * groups,)),
-            dma((3,)),
             dma((n_ang - 1, groups)),
             dma((n_ang - 1, groups)),
             dma((n_rad - 1, n_ang)),
@@ -380,9 +378,9 @@
             dma((n_ang - 1,)),
             dma((n_ang - 1,)),
         ],
-        compiler_params=pltpu.CompilerParams(collective_id=0, has_side_effects=True),
+        compiler_params=pltpu.CompilerParams(collective_id=0, has_side_effects=True, vmem_limit_bytes=52 << 20),
         name="moments",
-    )(density, forward[0], forward[1], weighted, jnp.asarray(packing.degrees()))
+    )(density, table)
     return pl.pallas_call(
         functools.partial(potential_kernel, packing, group),
         out_shape=jax.ShapeDtypeStruct(density.shape, jnp.float32),
@@ -393,6 +391,7 @@
             pltpu.VMEM((fields * groups, group, thetas, phis), jnp.float32),
             dma((fields * groups,)),
         ],
+        compiler_params=pltpu.CompilerParams(vmem_limit_bytes=52 << 20),
         name="potential",
     )(coef, jnp.asarray(legendre, jnp.float32), inverse[0], inverse[1])
 

time: 30.5 us -> 28.7 us (0.941)
  Pallas kernels: 30.3 us -> 27.4 us
  local copies, waits for them, and re-layouts: 0 us -> 1.1 us
    pallas_call x1, Pallas kernels: 23.4 us -> 21.7 us  [body(): pl.pallas_call(functools.partial(moments_kernel, n_rad, n_ang, packing, g...]
    pallas_call x1, Pallas kernels: 6.86 us -> 5.74 us  [body(): pl.pallas_call(functools.partial(potential_kernel, packing, group), out_s...]
    unnamed x0 -> x8, local copies, waits for them, and re-layouts: none -> 1.1 us
where the time goes in v3:
time: 28.7 us; the launch traced here: 28.5 us
  Pallas kernels  27.4 us (95%)
  local copies, waits for them, and re-layouts  1.1 us (4%)
    pallas_call x1, Pallas kernels, body(): pl.pallas_call(functools.partial(moments_kernel, n_rad, n_ang, packing, g...  21.7 us
    pallas_call x1, Pallas kernels, body(): pl.pallas_call(functools.partial(potential_kernel, packing, group), out_s...  5.74 us
    unnamed x8, local copies, waits for them, and re-layouts  1.1 us

profile of v3, /device:TPU:0, one launch (start us, length us, event | category | flops | bytes accessed | tf_op | source)
XLA Modules:
  0.0 28.5 jit_solution(16872886712571442565)
XLA Ops:
  0.0 0.0 copy-start
  0.0 1.1 %copy-done = f32[648,256]{1,0:T(8,128)S(1)} copy-done((f32[648,256]{1,0:T(8,128)S(1)}, f32[648,256]{1,0:T(8,128)}, u32[]{:S(2)}) %copy-start) | copy-done | bytes 663576
  1.1 0.0 copy-start.1
  1.1 0.0 copy-start.2
  1.1 0.0 copy-start.3
  1.1 21.7 %moments.1.coef = f32[4,64,128]{2,1,0:T(8,128)S(1)} custom-call(f32[3,64,32,512]{3,2,1,0:T(8,128)} %density.1, f32[648,256]{1,0:T(8,128)S(1)} %copy-done), custom_call_target="tpu_custom_call" | custom-call | tf_op jit(solution)/shard_map/moments/pallas_call | solution.py:358
  22.8 0.0 copy-done.1
  22.8 0.0 copy-done.2
  22.8 0.0 copy-done.3
  22.8 5.7 %potential.1 = f32[3,64,32,512]{3,2,1,0:T(8,128)} custom-call(f32[4,64,128]{2,1,0:T(8,128)S(1)} %moments.1.coef, f32[128,256]{1,0:T(8,128)S(1)} %copy-done.3, bf16[384,256]{1,0:T(8,128)(2,1)S(1)} %copy-done.2, bf16[384,256]{1,0:T(8,128)(2,1)S(1)} %copy-done.1), custom_call_target="tpu_custom_call" | custom-call | tf_op jit(solution)/shard_map/potential/pallas_call | solution.py:384
Async XLA Ops:
  0.0 1.1 %copy-start = (f32[648,256]{1,0:T(8,128)S(1)}, f32[648,256]{1,0:T(8,128)}, u32[]{:S(2)}) copy-start(f32[648,256]{1,0:T(8,128)} %constant.10.clone.table) | copy-start | bytes 1990660
  1.1 21.7 %copy-start.1 = (bf16[384,256]{1,0:T(8,128)(2,1)S(1)}, bf16[384,256]{1,0:T(8,128)(2,1)}, u32[]{:S(2)}) copy-start(bf16[384,256]{1,0:T(8,128)(2,1)} %constant.9.clone.odd_w) | copy-start | bytes 589828
  1.1 21.7 %copy-start.2 = (bf16[384,256]{1,0:T(8,128)(2,1)S(1)}, bf16[384,256]{1,0:T(8,128)(2,1)}, u32[]{:S(2)}) copy-start(bf16[384,256]{1,0:T(8,128)(2,1)} %constant.8.clone.even_w) | copy-start | bytes 589828
  1.1 21.7 %copy-start.3 = (f32[128,256]{1,0:T(8,128)S(1)}, f32[128,256]{1,0:T(8,128)}, u32[]{:S(2)}) copy-start(f32[128,256]{1,0:T(8,128)} %constant.11.clone.legendre) | copy-start | bytes 393220
